TPU v7x, 512 devices: a whole 4x4x16 slice. The times are simulated.
512 devices in a mesh: dp: 32 (over y, z_hi, core), tensor: 16 (over z_lo, x).
Axes of the slice: x: 4, y: 4, z: 16 (z_hi: 4, z_lo: 4; z = z_hi * 4 + z_lo), core: 2. Of those that a mesh axis runs over, the one named last changes fastest.
Arguments:
- acts: bfloat16 [12288, 4096], P('dp', 'tensor'), may hold values from -6 to 6
- grad_out: bfloat16 [12288, 4096], P('dp', 'tensor'), may hold values from -60 to 60
- gate_pre: bfloat16 [12288, 14336], P('dp', 'tensor'), may hold values from -6 to 6
- up_pre: bfloat16 [12288, 14336], P('dp', 'tensor'), may hold values from -6 to 6
- down_weight: bfloat16 [14336, 4096], P('tensor', 'dp'), may hold values from -0.09375 to 0.09375
- proj_in: bfloat16 [4096, 64], P('tensor'), may hold values from -0.09375 to 0.09375
- proj_out: bfloat16 [14336, 64], P('tensor'), may hold values from -0.046875 to 0.046875
- lengths: int32 [96], P('dp'), may hold values from 64 to 128
- query_ids: int32 [16], replicated, may hold values from 0 to 95
Outputs:
- gram: float32 [4096, 4096], P('dp', 'tensor')
- scores: float32 [16, 96], P(None, 'dp')
Inputs may be any that keep to these rules, and one draw needn't show every extreme that they name: `query_ids`: queries may repeat.
All inputs are finite; a program needn't handle non-finite values.
Results may differ from a plain program's by a relative error of at most 0.004.
Values may be sent and summed in bfloat16 or wider, within the bound.
No kernel may reach another device: no remote copies, remote signals or barrier semaphores. Data moves between devices by JAX's collectives and lax.ppermute only.
A program may use at most 64 MiB of HBM per device.

v0:
```python
import jax
import jax.numpy as jnp
from jax import lax
from jax.sharding import Mesh
from jax.sharding import PartitionSpec as P

TENSOR = ("tensor_0", "tensor_1")


def in_order(parts, dim):
    shape = list(parts.shape[1:])
    shape[dim] *= parts.shape[0]
    return jnp.moveaxis(parts, 0, dim).reshape(shape)


def stacked_from(array, axes, order):
    parts = array
    for k in order:
        parts = lax.all_gather(parts, axes[k])
    done = order[::-1]
    back = [done.index(k) for k in range(len(axes))]
    parts = parts.transpose(*back, *range(len(axes), parts.ndim))
    return parts.reshape(-1, *array.shape)


def whole_of(array, axes, order, dim):
    return in_order(stacked_from(array, axes, order), dim)


def filled_up(lines, count):
    spare = -len(lines) % count
    return jnp.pad(lines, [(0, spare)] + [(0, 0)] * (lines.ndim - 1))


def from_everyone(array, axis):
    count = lax.axis_size(axis)
    return lax.all_to_all(
        jnp.broadcast_to(array[None], (count, *array.shape)), axis, 0, 0, tiled=True
    )


def gather_directly(array, axis, dim):
    return in_order(from_everyone(array, axis), dim)


def split_up(array, dim, count):
    shape = array.shape
    parts = array.reshape(*shape[:dim], count, shape[dim] // count, *shape[dim + 1 :])
    return jnp.moveaxis(parts, dim, 0)


def sum_at_owner(array, axis, dim):
    count = lax.axis_size(axis)
    parts = lax.all_to_all(split_up(array, dim, count), axis, 0, 0, tiled=True)
    return jnp.sum(parts, axis=0)


def sum_by_parts(array, axes):
    padded = filled_up(array, lax.axis_size(axes))
    whole = gather_directly(sum_at_owner(padded, axes, 0), axes, 0)
    return lax.slice_in_dim(whole, 0, len(array)).reshape(array.shape)


def together(arrays, axis):
    flat, at, gathered = (jnp.concatenate([a.reshape(-1) for a in arrays]), 0, [])
    subtotal = sum_by_parts(flat, axis)
    for a in arrays:
        gathered.append(subtotal[at : at + a.size].reshape(a.shape))
        at += a.size
    return tuple(gathered)


def silu_slope(value):
    sigma = jax.nn.sigmoid(value)
    return sigma + value * sigma * (1.0 - sigma)


def body(acts, grad_out, gate_pre, up_pre, down_weight, proj_in, proj_out, lengths, query_ids):
    highest = lax.Precision.HIGHEST
    tokens_here = acts.shape[0]
    examples_here = lengths.shape[0]
    seq_len = tokens_here // examples_here
    full_grad = whole_of(grad_out, TENSOR, (0, 1), 1)
    hidden_grad = lax.dot_general(
        full_grad,
        lax.all_gather(down_weight, "dp", axis=1, tiled=True),
        (((1,), (1,)), ((), ())),
        preferred_element_type=jnp.float32,
    )
    gate_value = gate_pre.astype(jnp.float32)
    gate_grad = (hidden_grad * up_pre.astype(jnp.float32) * silu_slope(gate_value)).astype(
        jnp.bfloat16
    )
    out_part = jnp.dot(gate_grad, proj_out, preferred_element_type=jnp.float32)
    in_part = jnp.dot(acts, proj_in, preferred_element_type=jnp.float32)
    out_factor, in_factor = together((out_part, in_part), TENSOR)
    positions = lax.broadcasted_iota(jnp.int32, (examples_here, seq_len), 1)
    live = (positions < lengths[:, None]).astype(jnp.float32)
    out_factor = out_factor.reshape(examples_here, seq_len, -1) * live[:, :, None]
    in_factor = in_factor.reshape(examples_here, seq_len, -1)
    features = jnp.einsum("esa,esb->eab", out_factor, in_factor, precision=highest).reshape(
        examples_here, -1
    )
    width = features.shape[1]
    first_example = lax.axis_index("dp") * examples_here
    example_ids = first_example + lax.broadcasted_iota(jnp.int32, (1, examples_here), 1)
    selector = (query_ids[:, None] == example_ids).astype(jnp.float32)
    query_part = jnp.dot(selector, features, precision=highest)
    local_square = jnp.sum(features * features)
    query_feat, total_square = together((query_part, local_square), "dp")
    examples_all = examples_here * lax.axis_size("dp")
    norm_mean = total_square / examples_all + 1e-06
    col_width = width // lax.axis_size(TENSOR)
    own_cols = lax.dynamic_slice_in_dim(features, lax.axis_index(TENSOR) * col_width, col_width, 1)
    row_block = lax.all_to_all(features, "dp", split_axis=1, concat_axis=0, tiled=True)
    block = lax.dot_general(
        row_block,
        gather_directly(own_cols, "dp", 0),
        (((0,), (0,)), ((), ())),
        precision=highest,
        preferred_element_type=jnp.float32,
    )
    gram = block * (width / examples_all) / norm_mean
    scores = jnp.dot(query_feat, features.T, precision=highest) / norm_mean
    return (gram, scores)


def solution(mesh):
    split = Mesh(mesh.devices.reshape(mesh.shape["dp"], 4, 4), ("dp", "tensor_0", "tensor_1"))
    in_specs = (
        P("dp", TENSOR),
        P("dp", TENSOR),
        P("dp", TENSOR),
        P("dp", TENSOR),
        P(TENSOR, "dp"),
        P(TENSOR, None),
        P(TENSOR, None),
        P("dp"),
        P(),
    )
    out_specs = (P("dp", TENSOR), P(None, "dp"))
    return jax.shard_map(body, mesh=split, in_specs=in_specs, out_specs=out_specs, check_vma=False)
```

profile of v0, /device:TPU:1, one launch (start us, length us, event | category | flops | bytes accessed | tf_op | source)
XLA Modules:
  0.0 366.1 jit_solution(10889218226166880357)
XLA Ops:
  7.2 20.1 %all-gather = bf16[1536,256]{1,0:T(8,128)(2,1)} all-gather(bf16[384,256]{1,0:T(8,128)(2,1)} %param.10), channel_id=2, replica_groups=mesh['dp'=32,'tensor_0'=4,'tensor_1'=4] {'tensor_0'}, dimensions={0}, use_global_device_ids=true | all-gather | bytes 983040 | tf_op jit(solution)/shard_map/all_gather | solution.py:19
  27.4 0.7 all-gather.5.cloned.1.call-update
  28.4 50.3 %all-gather.7.cloned.1.call-done = bf16[16,384,256]{2,1,0:T(8,128)(2,1)} async-done(((bf16[4,384,256]{2,1,0:T(8,128)(2,1)}), bf16[16,384,256]{2,1,0:T(8,128)(2,1)}) %all-gather.7.cloned.1.call-update) | async-done | bytes 3145744 | tf_op jit(solution)/shard_map/all_gather | solution.py:19
  78.7 2.1 copy.42
  80.8 2.8 copy.43
  83.6 132.9 %all-gather.5.cloned.1.call-done = bf16[896,4096]{1,0:T(8,128)(2,1)} async-done(((bf16[896,128]{1,0:T(8,128)(2,1)}), bf16[896,4096]{1,0:T(8,128)(2,1)}) %all-gather.5.cloned.1.call-update) | async-done | bytes 7340048 | tf_op jit(solution)/shard_map/all_gather | solution.py:86
  216.5 8.0 %fusion.7 = f32[384,64]{1,0:T(8,128)S(1)} fusion(bf16[896,64]{0,1:T(8,128)(2,1)} %param.15, bf16[384,896]{1,0:T(8,128)(2,1)} %param.11, bf16[384,896]{1,0:T(8,128)(2,1)} %param.12, bf16[384,4096]{0,1:T(8,128)(2,1)} %bitcast.35, bf16[896,4096]{1,0:T(8,128)(2,1)} %all-gather.5.cloned.1.call-done), kind=kOutput, calls=%fused_computation.11 | convolution fusion | flops 2866741248 | bytes 12075008 | tf_op jit(solution)/shard_map/dot_general | solution.py:94
  224.6 0.2 copy.46
  224.8 12.5 %all_to_all.51 = f32[16,1,3072]{2,1,0:T(1,128)S(1)} all-to-all(f32[16,1,3072]{2,1,0:T(1,128)S(1)} %copy.46), channel_id=1, replica_groups=mesh['dp'=32,'tensor_0'=4,'tensor_1'=4] {'tensor_0','tensor_1'}, dimensions={0} | all-to-all | bytes 393216 | tf_op jit(solution)/shard_map/all_to_all | solution.py:54
  237.4 0.8 broadcast_in_dim.6
  238.2 3.9 %all-to-all-start.1 = ((f32[16,1,3072]{2,1,0:T(1,128)}), f32[16,1,3072]{2,1,0:T(1,128)S(1)}, u32[]{:S(2)}, u32[]{:S(2)}) async-start(f32[16,1,3072]{2,1,0:T(1,128)} %broadcast_in_dim.6), calls=%async_computation.1 | async-start | bytes 393216 | tf_op jit(solution)/shard_map/all_to_all | solution.py:37
  242.2 8.2 %all-to-all-done.1 = f32[16,1,3072]{2,1,0:T(1,128)S(1)} async-done(((f32[16,1,3072]{2,1,0:T(1,128)}), f32[16,1,3072]{2,1,0:T(1,128)S(1)}, u32[]{:S(2)}, u32[]{:S(2)}) %all-to-all-start.1) | async-done | bytes 196640 | tf_op jit(solution)/shard_map/all_to_all | solution.py:37
  250.4 0.5 slice_reduce_fusion.1
  251.1 1.2 multiply_reduce_fusion
  252.4 0.3 convolution_bitcast_fusion
  252.8 0.7 select_maximum_fusion
  253.4 1.1 all_to_all.42
  254.5 11.2 %all-to-all-start.4 = ((f32[32,1,2049]{2,1,0:T(1,128)}), f32[32,1,2049]{2,1,0:T(1,128)S(1)}, u32[]{:S(2)}, u32[]{:S(2)}) async-start(f32[32,1,2049]{2,1,0:T(1,128)} %all_to_all.42), calls=%async_computation.4 | async-start | bytes 557056 | tf_op jit(solution)/shard_map/all_to_all | solution.py:54
  265.8 0.7 copy.49
  266.5 19.6 %all-to-all-done.4 = f32[32,1,2049]{2,1,0:T(1,128)S(1)} async-done(((f32[32,1,2049]{2,1,0:T(1,128)}), f32[32,1,2049]{2,1,0:T(1,128)S(1)}, u32[]{:S(2)}, u32[]{:S(2)}) %all-to-all-start.4) | async-done | bytes 262304 | tf_op jit(solution)/shard_map/all_to_all | solution.py:54
  286.1 7.2 %all-to-all-start.2 = ((f32[3,32,128]{2,0,1:T(4,128)}), f32[3,32,128]{2,0,1:T(4,128)S(1)}, u32[]{:S(2)}, u32[]{:S(2)}) async-start(f32[3,32,128]{2,0,1:T(4,128)} %copy.49), calls=%async_computation.2 | async-start | bytes 131072 | tf_op jit(solution)/shard_map/all_to_all | solution.py:115
  293.4 14.8 %all-to-all-done.2 = f32[3,32,128]{2,0,1:T(4,128)S(1)} async-done(((f32[3,32,128]{2,0,1:T(4,128)}), f32[3,32,128]{2,0,1:T(4,128)S(1)}, u32[]{:S(2)}, u32[]{:S(2)}) %all-to-all-start.2) | async-done | bytes 49184 | tf_op jit(solution)/shard_map/all_to_all | solution.py:115
  308.2 0.9 broadcast_in_dim.8
  309.1 3.8 %all-to-all-start.5 = ((f32[32,1,2049]{2,1,0:T(1,128)}), f32[32,1,2049]{2,1,0:T(1,128)S(1)}, u32[]{:S(2)}, u32[]{:S(2)}) async-start(f32[32,1,2049]{2,1,0:T(1,128)} %broadcast_in_dim.8), calls=%async_computation.5 | async-start | bytes 557056 | tf_op jit(solution)/shard_map/all_to_all | solution.py:37
  312.9 17.7 %all-to-all-done.5 = f32[32,1,2049]{2,1,0:T(1,128)S(1)} async-done(((f32[32,1,2049]{2,1,0:T(1,128)}), f32[32,1,2049]{2,1,0:T(1,128)S(1)}, u32[]{:S(2)}, u32[]{:S(2)}) %all-to-all-start.5) | async-done | bytes 262304 | tf_op jit(solution)/shard_map/all_to_all | solution.py:37
  330.6 0.7 broadcast_in_dim.7
  331.3 9.4 %all-to-all-start.3 = ((f32[32,3,256]{2,1,0:T(4,128)}), f32[32,3,256]{2,1,0:T(4,128)S(1)}, u32[]{:S(2)}, u32[]{:S(2)}) async-start(f32[32,3,256]{2,1,0:T(4,128)} %broadcast_in_dim.7), calls=%async_computation.3 | async-start | bytes 262144 | tf_op jit(solution)/shard_map/all_to_all | solution.py:37
  340.7 0.7 reduce.5
  341.5 0.5 slice.25
  342.8 1.0 convolution_divide_fusion
  343.8 14.5 %all-to-all-done.3 = f32[32,3,256]{2,1,0:T(4,128)S(1)} async-done(((f32[32,3,256]{2,1,0:T(4,128)}), f32[32,3,256]{2,1,0:T(4,128)S(1)}, u32[]{:S(2)}, u32[]{:S(2)}) %all-to-all-start.3) | async-done | bytes 98336 | tf_op jit(solution)/shard_map/all_to_all | solution.py:37
  358.3 1.0 fusion.9
  (28 shorter events, 1.6 us)
Async XLA Ops:
  7.2 20.9 %copy-start = (bf16[384,256]{1,0:T(8,128)(2,1)S(1)}, bf16[384,256]{1,0:T(8,128)(2,1)}, u32[]{:S(2)}) copy-start(bf16[384,256]{1,0:T(8,128)(2,1)} %param.9) | copy-start | bytes 589828
  7.2 20.9 %copy-start.1 = (bf16[256,64]{0,1:T(8,128)(2,1)S(1)}, bf16[256,64]{0,1:T(8,128)(2,1)}, u32[]{:S(2)}) copy-start(bf16[256,64]{0,1:T(8,128)(2,1)} %param.14) | copy-start | bytes 98308
  7.2 71.5 %all-gather.7.cloned.1.call-start = ((), (), s32[]{:S(2)}) async-start(), calls=%async_computation.7 | async-start | bytes 3932160 | tf_op jit(solution)/shard_map/all_gather | solution.py:19
  27.3 189.2 %all-gather.5.cloned.1.call-start = ((), (), s32[]{:S(2)}) async-start(), calls=%async_computation.6 | async-start | bytes 7569408 | tf_op jit(solution)/shard_map/all_gather | solution.py:86
  224.5 17.7 %copy-start.3 = (s32[3]{0:T(128)S(1)}, s32[3]{0:T(128)}, u32[]{:S(2)}) copy-start(s32[3]{0:T(128)} %param.16) | copy-start | bytes 40
  224.8 27.6 %copy-start.2 = (s32[16]{0:T(128)S(1)}, s32[16]{0:T(128)}, u32[]{:S(2)}) copy-start(s32[16]{0:T(128)} %param.17) | copy-start | bytes 196
  238.2 12.2 %all-to-all-start.1 = ((f32[16,1,3072]{2,1,0:T(1,128)}), f32[16,1,3072]{2,1,0:T(1,128)S(1)}, u32[]{:S(2)}, u32[]{:S(2)}) async-start(f32[16,1,3072]{2,1,0:T(1,128)} %broadcast_in_dim.6), calls=%async_computation.1 | async-start | bytes 393216 | tf_op jit(solution)/shard_map/all_to_all | solution.py:37
  254.5 31.5 %all-to-all-start.4 = ((f32[32,1,2049]{2,1,0:T(1,128)}), f32[32,1,2049]{2,1,0:T(1,128)S(1)}, u32[]{:S(2)}, u32[]{:S(2)}) async-start(f32[32,1,2049]{2,1,0:T(1,128)} %all_to_all.42), calls=%async_computation.4 | async-start | bytes 557056 | tf_op jit(solution)/shard_map/all_to_all | solution.py:54
  286.1 22.1 %all-to-all-start.2 = ((f32[3,32,128]{2,0,1:T(4,128)}), f32[3,32,128]{2,0,1:T(4,128)S(1)}, u32[]{:S(2)}, u32[]{:S(2)}) async-start(f32[3,32,128]{2,0,1:T(4,128)} %copy.49), calls=%async_computation.2 | async-start | bytes 131072 | tf_op jit(solution)/shard_map/all_to_all | solution.py:115
  309.1 21.5 %all-to-all-start.5 = ((f32[32,1,2049]{2,1,0:T(1,128)}), f32[32,1,2049]{2,1,0:T(1,128)S(1)}, u32[]{:S(2)}, u32[]{:S(2)}) async-start(f32[32,1,2049]{2,1,0:T(1,128)} %broadcast_in_dim.8), calls=%async_computation.5 | async-start | bytes 557056 | tf_op jit(solution)/shard_map/all_to_all | solution.py:37
  331.3 27.0 %all-to-all-start.3 = ((f32[32,3,256]{2,1,0:T(4,128)}), f32[32,3,256]{2,1,0:T(4,128)S(1)}, u32[]{:S(2)}, u32[]{:S(2)}) async-start(f32[32,3,256]{2,1,0:T(4,128)} %broadcast_in_dim.7), calls=%async_computation.3 | async-start | bytes 262144 | tf_op jit(solution)/shard_map/all_to_all | solution.py:37
Sparse Core Ops, SparseCore 0:
  27.4 51.1 all-gather.6
  81.7 134.7 all-gather.4
where the time goes:
time: 367 us; the launch traced here: 366 us
  waiting for transfers between devices  259 us (71%)
  starting transfers between devices  35.5 us (10%)
  blocking collectives  32.5 us (9%)
  between operations  14.9 us (4%)
  matrix products  11.6 us (3%)
  local copies, waits for them, and re-layouts  11.1 us (3%)
    all_gather x1, waiting for transfers between devices, body(): lax.all_gather(down_weight, 'dp', axis=1, tiled=True)  133 us
    all_gather x1, waiting for transfers between devices, stacked_from(): parts = lax.all_gather(parts, axes[k])  50.3 us
    all_to_all x3, waiting for transfers between devices, from_everyone(): lax.all_to_all(jnp.broadcast_to(array[None], (count, *array.shape)), axis...  40.4 us
    all_gather x1, blocking collectives, stacked_from(): parts = lax.all_gather(parts, axes[k])  20.1 us
    all_to_all x1, waiting for transfers between devices, sum_at_owner(): parts = lax.all_to_all(split_up(array, dim, count), axis, 0, 0, tiled=True)  19.6 us
    all_to_all x3, starting transfers between devices, from_everyone(): lax.all_to_all(jnp.broadcast_to(array[None], (count, *array.shape)), axis...  17.1 us
    all_to_all x1, waiting for transfers between devices, body(): lax.all_to_all(features, 'dp', split_axis=1, concat_axis=0, tiled=True)  14.8 us
    all_to_all x1, blocking collectives, sum_at_owner(): parts = lax.all_to_all(split_up(array, dim, count), axis, 0, 0, tiled=True)  12.5 us
  transfers between devices with their start and end apart: 7, of which 7 were waited for; matrix products, arithmetic and copies ran while one was open for 2% of the time, Pallas kernels for 0%

commit v1 on v0

v1 whole, which is shorter than its diff:
```python
import functools

import jax
import jax.numpy as jnp
from jax import lax
from jax.experimental import pallas as pl
from jax.experimental.pallas import tpu as pltpu
from jax.sharding import Mesh
from jax.sharding import PartitionSpec as P


DP = ("y", "zh", "c")
TENSOR = ("zl", "x")
F32 = jnp.float32
BF16 = jnp.bfloat16
HIGH = lax.Precision.HIGHEST
NT = (((1,), (1,)), ((), ()))
VM = pl.BlockSpec(memory_space=pltpu.VMEM)
SM = pl.BlockSpec(memory_space=pltpu.SMEM)
ANY = pl.BlockSpec(memory_space=pl.ANY)


def shift(value, axis, by):
    count = lax.axis_size(axis)
    return lax.ppermute(value, axis, [(k, (k + by) % count) for k in range(count)])


def exchange(value, axis):
    return lax.all_to_all(value, axis, 0, 0, tiled=True)


def pack_rows(msg_ref, table, examples, per):
    seq = table.shape[1] // examples
    for j in range(msg_ref.shape[0]):
        for e in range(examples):
            msg_ref[j, e * per : (e + 1) * per, :] = table[
                j * per : (j + 1) * per, e * seq : (e + 1) * seq
            ]
        if msg_ref.shape[1] > examples * per:
            rest = msg_ref.shape[1] - examples * per
            msg_ref[j, examples * per :, :] = jnp.zeros((rest, seq), F32)


def in_kernel(examples, per, proj_ref, acts_ref, msg_ref):
    table = lax.dot_general(proj_ref[...], acts_ref[...], NT, preferred_element_type=F32)
    pack_rows(msg_ref, table, examples, per)


def slope_kernel(gate_ref, up_ref, out_ref):
    value = gate_ref[...].astype(F32)
    sigma = jax.nn.sigmoid(value)
    out_ref[...] = up_ref[...].astype(F32) * (sigma + value * sigma * (1.0 - sigma))


def times(ws, gs, g):
    left = jnp.concatenate([gs[g, z] for z in range(4)], axis=1)
    right = jnp.concatenate([ws[g, c, z] for z in range(4) for c in range(2)], axis=1)
    return lax.dot_general(left, right, NT, preferred_element_type=F32)


def most_kernel(where, w0, w1, w2, v0, v1, v2, g0, g1, g2, g3, acc_ref, ws, gs, sems):
    y, c = where[0], where[2]
    copies = []
    for g, (mine, other, step) in enumerate(((w0, v0, 0), (w1, v1, 3), (w2, v2, 1))):
        copies.append(
            [
                pltpu.make_async_copy(mine, ws.at[g, c], sems.at[g, 0]),
                pltpu.make_async_copy(other, ws.at[g, 1 - c], sems.at[g, 1]),
            ]
            + [
                pltpu.make_async_copy(
                    ref.at[lax.rem(y + step, 4)], gs.at[g, lax.rem(where[4] + k, 4)], sems.at[g, 2 + k]
                )
                for k, ref in enumerate((g0, g1, g2, g3))
            ]
        )
    for group in copies:
        for copy in group:
            copy.start()
    for g, group in enumerate(copies):
        for copy in group:
            copy.wait()
        part = times(ws, gs, g)
        acc_ref[...] = part if g == 0 else acc_ref[...] + part


def last_kernel(
    examples, per, where, q0, q1, r0, r1, g0, g1, g2, g3, acc_ref, slope_ref, proj_ref, msg_ref, ws, gs, sems
):
    y, c = where[0], where[2]
    copies = [
        pltpu.make_async_copy(q0, ws.at[0, c, pl.ds(0, 2)], sems.at[0]),
        pltpu.make_async_copy(q1, ws.at[0, c, pl.ds(2, 2)], sems.at[1]),
        pltpu.make_async_copy(r0, ws.at[0, 1 - c, pl.ds(0, 2)], sems.at[2]),
        pltpu.make_async_copy(r1, ws.at[0, 1 - c, pl.ds(2, 2)], sems.at[3]),
    ] + [
        pltpu.make_async_copy(
            ref.at[lax.rem(y + 2, 4)], gs.at[0, lax.rem(where[4] + k, 4)], sems.at[4 + k]
        )
        for k, ref in enumerate((g0, g1, g2, g3))
    ]
    for copy in copies:
        copy.start()
    for copy in copies:
        copy.wait()
    hidden = acc_ref[...] + times(ws, gs, 0)
    gate_grad = (hidden * slope_ref[...]).astype(BF16)
    table = lax.dot_general(proj_ref[...], gate_grad, NT, preferred_element_type=F32)
    pack_rows(msg_ref, table, examples, per)


def feature_kernel(examples, per, lengths, out_ref, in_ref, msg_ref):
    rows = jnp.sum(out_ref[...], axis=0)
    seq = rows.shape[1]
    position = lax.broadcasted_iota(jnp.int32, (per, seq), 1)
    lines = []
    for e in range(examples):
        left = jnp.where(position < lengths[e], rows[e * per : (e + 1) * per], 0.0)
        right = jnp.concatenate(
            [in_ref[j, e * per : (e + 1) * per, :] for j in range(in_ref.shape[0])], axis=0
        )
        part = lax.dot_general(left, right, NT, precision=HIGH, preferred_element_type=F32)
        for h in range(per // 2):
            lines.append(jnp.concatenate([part[2 * h : 2 * h + 1], part[2 * h + 1 : 2 * h + 2]], axis=1))
    lines.append(jnp.zeros((msg_ref.shape[1] - len(lines), 2 * part.shape[1]), F32))
    tile = jnp.concatenate(lines, axis=0)
    msg_ref[...] = jnp.broadcast_to(tile[None], msg_ref.shape)


def columns_of(all_ref, examples):
    return jnp.concatenate(
        [
            jnp.concatenate([all_ref[:, 2 * e, :], all_ref[:, 2 * e + 1, :]], axis=1)
            for e in range(examples)
        ],
        axis=0,
    )


def share_kernel(examples, where, pick_ref, all_ref, col_ref, msg_ref):
    cols = columns_of(all_ref, examples)
    col_ref[...] = cols
    count = cols.shape[0]
    half = cols.shape[1] // 2
    own = all_ref[where[5]]
    chosen = (
        pick_ref[...] == lax.broadcasted_iota(jnp.int32, (pick_ref.shape[0], count), 1)
    ).astype(F32)
    asked = jnp.dot(chosen, cols, precision=HIGH, preferred_element_type=F32)
    score = jnp.zeros((asked.shape[0], 128), F32)
    lane = lax.broadcasted_iota(jnp.int32, score.shape, 1)
    for e in range(examples):
        row = jnp.concatenate([own[2 * e : 2 * e + 1], own[2 * e + 1 : 2 * e + 2]], axis=1)
        value = jnp.sum(asked * row, axis=1, keepdims=True)
        score = jnp.where(lane == e, value, score)
    square = jnp.sum(jnp.sum(cols * cols, axis=1, keepdims=True), axis=0, keepdims=True)
    score = jnp.where(lane == examples, square, score)
    high = score.astype(BF16).astype(F32)
    low = score - high
    both = jnp.where(lane < 64, high, pltpu.roll(low, 64, 1)).astype(BF16)
    rows = jnp.where(lax.rem(where[5], 2) == 0, cols[:, :half], cols[:, half:]).astype(BF16)
    tile = jnp.concatenate([rows, both], axis=0)
    for j in range(msg_ref.shape[0]):
        msg_ref[j] = tile


def gram_kernel(examples, where, all_ref, col_ref, gram_ref, score_ref):
    cols = col_ref[...]
    count, width = cols.shape
    rows = all_ref[lax.div(where[5], 2), :count, :].astype(F32)
    both = jnp.sum(all_ref[:, count:, :].astype(F32), axis=0)
    score = both + pltpu.roll(both, 64, 1)
    total = score[0:1, examples : examples + 1]
    norm = total / count + 1e-06
    block = lax.dot_general(
        rows, cols, (((0,), (0,)), ((), ())), precision=HIGH, preferred_element_type=F32
    )
    gram_ref[...] = block * (width * all_ref.shape[0] / count) / norm
    score_ref[...] = (score / norm)[:, :examples]


def step(acts, grad_out, gate_pre, up_pre, down_weight, proj_in, proj_out, lengths, query_ids):
    tokens, ff_here = gate_pre.shape
    examples = lengths.shape[0]
    tensor = lax.axis_size(TENSOR)
    groups = lax.axis_size(DP)
    ko = proj_out.shape[1]
    per = ko // tensor
    index = [lax.axis_index(a) for a in ("y", "zh", "c", "zl", "x")]
    where = jnp.stack(index + [lax.axis_index(DP)]).astype(jnp.int32)
    msg = jax.ShapeDtypeStruct((tensor, 16, 128), F32)

    gz = lax.all_gather(grad_out, "zl")
    gz, down_weight = lax.optimization_barrier((gz, down_weight))
    wz = lax.all_gather(down_weight, "zh")
    gx = [gz]
    for k in (1, 2, 3):
        gx.append(shift(gz, "x", -k))
    wp = shift(wz, "y", 1)
    wm = shift(wz, "y", -1)
    q0 = shift(wp[:2], "y", 1)
    q1 = shift(wm[2:], "y", -1)
    cz, cp, cm = shift(wz, "c", 1), shift(wp, "c", 1), shift(wm, "c", 1)
    r0, r1 = shift(q0, "c", 1), shift(q1, "c", 1)

    in_msg = pl.pallas_call(
        functools.partial(in_kernel, examples, per), out_shape=msg, in_specs=[VM, VM], out_specs=VM
    )(proj_in.T, acts)
    in_own = jnp.sum(exchange(in_msg, TENSOR), axis=0)
    in_all = exchange(jnp.broadcast_to(in_own[None], (tensor, *in_own.shape)), TENSOR)
    slope = pl.pallas_call(
        slope_kernel,
        out_shape=jax.ShapeDtypeStruct((tokens, ff_here), F32),
        in_specs=[VM, VM],
        out_specs=VM,
    )(gate_pre, up_pre)
    gshape = (4, tokens, grad_out.shape[1])
    wshape = (2, 4, *down_weight.shape)
    acc = pl.pallas_call(
        most_kernel,
        out_shape=jax.ShapeDtypeStruct((tokens, ff_here), F32),
        in_specs=[SM] + [ANY] * 10,
        out_specs=VM,
        scratch_shapes=[
            pltpu.VMEM((3, *wshape), BF16),
            pltpu.VMEM((3, *gshape), BF16),
            pltpu.SemaphoreType.DMA((3, 6)),
        ],
    )(where, wz, wp, wm, cz, cp, cm, *gx)
    out_msg = pl.pallas_call(
        functools.partial(last_kernel, examples, per),
        out_shape=msg,
        in_specs=[SM] + [ANY] * 8 + [VM] * 3,
        out_specs=VM,
        scratch_shapes=[
            pltpu.VMEM((1, *wshape), BF16),
            pltpu.VMEM((1, *gshape), BF16),
            pltpu.SemaphoreType.DMA((8,)),
        ],
    )(where, q0, q1, r0, r1, *gx, acc, slope, proj_out.T)
    out_all = exchange(out_msg, TENSOR)
    piece = pl.pallas_call(
        functools.partial(feature_kernel, examples, per),
        out_shape=jax.ShapeDtypeStruct((groups, 8, 128), F32),
        in_specs=[SM, VM, VM],
        out_specs=VM,
    )(lengths, out_all, in_all)
    pieces = exchange(piece, DP)
    count = examples * groups
    pick = ((query_ids % examples) * groups + query_ids // examples)[:, None]
    queries = query_ids.shape[0]
    cols, row_msg = pl.pallas_call(
        functools.partial(share_kernel, examples),
        out_shape=(
            jax.ShapeDtypeStruct((count, 256), F32),
            jax.ShapeDtypeStruct((tensor, count + queries, 128), BF16),
        ),
        in_specs=[SM, VM, VM],
        out_specs=(VM, VM),
    )(where, pick, pieces)
    row_all = exchange(row_msg, TENSOR)
    gram, scores = pl.pallas_call(
        functools.partial(gram_kernel, examples),
        out_shape=(
            jax.ShapeDtypeStruct((128, 256), F32),
            jax.ShapeDtypeStruct((queries, examples), F32),
        ),
        in_specs=[SM, VM, VM],
        out_specs=(VM, VM),
    )(where, row_all, cols)
    return gram, scores


def solution(mesh):
    split = Mesh(mesh.devices.reshape(4, 4, 2, 4, 4), (*DP, *TENSOR))
    in_specs = (
        P(DP, TENSOR),
        P(DP, TENSOR),
        P(DP, TENSOR),
        P(DP, TENSOR),
        P(TENSOR, DP),
        P(TENSOR, None),
        P(TENSOR, None),
        P(DP),
        P(),
    )
    out_specs = (P(DP, TENSOR), P(None, DP))
    return jax.shard_map(step, mesh=split, in_specs=in_specs, out_specs=out_specs, check_vma=False)
```

time: 367 us -> 214 us (0.58)
  waiting for transfers between devices: 259 us -> 18.6 us
  blocking collectives: 32.5 us -> 91.9 us
  starting transfers between devices: 35.5 us -> 70.6 us
  Pallas kernels: 0 us -> 22.5 us
  between operations: 14.9 us -> 0.9 us
  matrix products: 11.6 us -> 0 us
    all_gather x2 -> x0, waiting for transfers between devices: 183 us -> none  [the longest x1 133 us: body(): lax.all_gather(down_weight, 'dp', axis=1, tiled=True)]
    all_to_all x5 -> x3, waiting for transfers between devices: 74.8 us -> 15.1 us  [exchange(): return lax.all_to_all(value, axis, 0, 0, tiled=True)]
    ppermute x0 -> x12, starting transfers between devices: none -> 50.5 us  [shift(): lax.ppermute(value, axis, [(k, (k + by) % count) for k in range(count)])]
    all_gather x1 -> x2, blocking collectives: 20.1 us -> 60.9 us  [the longest x1 41.5 us: step(): wz = lax.all_gather(down_weight, 'zh')]
    pallas_call x0 -> x7, Pallas kernels: none -> 22.5 us  [the longest x1 6.4 us: step(): pl.pallas_call(most_kernel, out_shape=jax.ShapeDtypeStruct((tokens, ff_he...]
    all_to_all x1 -> x2, blocking collectives: 12.5 us -> 31 us  [exchange(): return lax.all_to_all(value, axis, 0, 0, tiled=True)]
    all_to_all x5 -> x3, starting transfers between devices: 35.5 us -> 20.1 us  [exchange(): return lax.all_to_all(value, axis, 0, 0, tiled=True)]
    dot_general x6 -> x0, matrix products: 11.6 us -> none  [the longest x1 7.97 us: body(): out_part = jnp.dot(gate_grad, proj_out, preferred_element_type=jnp.float32)]
  transfers between devices with their start and end apart: 7 -> 15, of which waited for: 7 -> 4; matrix products, arithmetic and copies ran while one was open for 2% -> 3% of each run, Pallas kernels for 0% -> 8%
where the time goes in v1:
time: 214 us; the launch traced here: 213 us
  blocking collectives  91.9 us (43%)
  starting transfers between devices  70.6 us (33%)
  Pallas kernels  22.5 us (11%)
  waiting for transfers between devices  18.6 us (9%)
  local copies, waits for them, and re-layouts  8.48 us (4%)
    ppermute x12, starting transfers between devices, shift(): lax.ppermute(value, axis, [(k, (k + by) % count) for k in range(count)])  50.5 us
    all_gather x1, blocking collectives, step(): wz = lax.all_gather(down_weight, 'zh')  41.5 us
    all_to_all x2, blocking collectives, exchange(): return lax.all_to_all(value, axis, 0, 0, tiled=True)  31 us
    all_to_all x3, starting transfers between devices, exchange(): return lax.all_to_all(value, axis, 0, 0, tiled=True)  20.1 us
    all_gather x1, blocking collectives, step(): gz = lax.all_gather(grad_out, 'zl')  19.4 us
    all_to_all x3, waiting for transfers between devices, exchange(): return lax.all_to_all(value, axis, 0, 0, tiled=True)  15.1 us
    pallas_call x1, Pallas kernels, step(): pl.pallas_call(most_kernel, out_shape=jax.ShapeDtypeStruct((tokens, ff_he...  6.4 us
    pallas_call x1, Pallas kernels, step(): pl.pallas_call(functools.partial(last_kernel, examples, per), out_shape=m...  5.35 us
  transfers between devices with their start and end apart: 15, of which 4 were waited for; matrix products, arithmetic and copies ran while one was open for 3% of the time, Pallas kernels for 8%

profile of v1, /device:TPU:1, one launch (start us, length us, event | category | flops | bytes accessed | tf_op | source)
XLA Modules:
  0.0 213.1 jit_solution(15859497535343898059)
XLA Ops:
  0.6 19.4 %all-gather = bf16[1536,256]{1,0:T(8,128)(2,1)S(1)} all-gather(bf16[384,256]{1,0:T(8,128)(2,1)} %param.10), channel_id=2, replica_groups=mesh['y'=4,'zh'=4,'c'=2,'zl'=4,'x'=4] {'zl'}, dimensions={0}, use_global_device_ids=true | all-gather | bytes 983040 | tf_op jit(solution)/shard_map/all_gather | solution.py:193
  20.1 41.5 %all-gather.1 = bf16[3584,128]{1,0:T(8,128)(2,1)S(1)} all-gather(bf16[896,128]{1,0:T(8,128)(2,1)} %param.13), channel_id=3, replica_groups=mesh['y'=4,'zh'=4,'c'=2,'zl'=4,'x'=4] {'zh'}, dimensions={0}, use_global_device_ids=true | all-gather | bytes 1146880 | tf_op jit(solution)/shard_map/all_gather | solution.py:195
  61.6 3.2 %collective-permute-start = (bf16[4,896,128]{2,1,0:T(8,128)(2,1)S(1)}, bf16[4,896,128]{2,1,0:T(8,128)(2,1)}, u32[]{:S(2)}, u32[]{:S(2)}) collective-permute-start(bf16[4,896,128]{2,1,0:T(8,128)(2,1)S(1)} %bitcast.17), channel_id=1, source_target_pairs={{0,128},{128,256},{256,384},{384,0},{1,129},{129,257},{257,385},{3... | collective-permute-start | bytes 2752520 | tf_op jit(solution)/shard_map/ppermute | solution.py:25
  64.8 3.4 %collective-permute-start.2 = (bf16[4,896,128]{2,1,0:T(8,128)(2,1)S(1)}, bf16[4,896,128]{2,1,0:T(8,128)(2,1)}, u32[]{:S(2)}, u32[]{:S(2)}) collective-permute-start(bf16[4,896,128]{2,1,0:T(8,128)(2,1)S(1)} %bitcast.18), channel_id=1, source_target_pairs={{0,384},{128,0},{256,128},{384,256},{1,385},{129,1},{257,129},{385... | collective-permute-start | bytes 2752520 | tf_op jit(solution)/shard_map/ppermute | solution.py:25
  68.2 4.4 %collective-permute-start.6 = (bf16[4,384,256]{2,1,0:T(8,128)(2,1)S(1)}, bf16[4,384,256]{2,1,0:T(8,128)(2,1)S(1)}, u32[]{:S(2)}, u32[]{:S(2)}) collective-permute-start(bf16[4,384,256]{2,1,0:T(8,128)(2,1)S(1)} %bitcast.12), channel_id=1, source_target_pairs={{0,3},{1,0},{2,1},{3,2},{4,7},{5,4},{6,5},{7,6},{8,11},{9,8},{10,9... | collective-permute-start | bytes 2359304 | tf_op jit(solution)/shard_map/ppermute | solution.py:25
  72.5 2.4 %collective-permute-start.7 = (bf16[4,384,256]{2,1,0:T(8,128)(2,1)S(1)}, bf16[4,384,256]{2,1,0:T(8,128)(2,1)S(1)}, u32[]{:S(2)}, u32[]{:S(2)}) collective-permute-start(bf16[4,384,256]{2,1,0:T(8,128)(2,1)S(1)} %bitcast.13), channel_id=1, source_target_pairs={{0,2},{1,3},{2,0},{3,1},{4,6},{5,7},{6,4},{7,5},{8,10},{9,11},{10,... | collective-permute-start | bytes 2359304 | tf_op jit(solution)/shard_map/ppermute | solution.py:25
  75.0 2.5 %collective-permute-start.8 = (bf16[4,384,256]{2,1,0:T(8,128)(2,1)S(1)}, bf16[4,384,256]{2,1,0:T(8,128)(2,1)}, u32[]{:S(2)}, u32[]{:S(2)}) collective-permute-start(bf16[4,384,256]{2,1,0:T(8,128)(2,1)S(1)} %bitcast.14), channel_id=1, source_target_pairs={{0,1},{1,2},{2,3},{3,0},{4,5},{5,6},{6,7},{7,4},{8,9},{9,10},{10,1... | collective-permute-start | bytes 2359304 | tf_op jit(solution)/shard_map/ppermute | solution.py:25
  77.5 1.8 shard_map.107
  79.3 4.2 %all-to-all-start.1 = ((f32[16,16,128]{2,1,0:T(8,128)}), f32[16,16,128]{2,1,0:T(8,128)S(1)}, u32[]{:S(2)}, u32[]{:S(2)}) async-start(f32[16,16,128]{2,1,0:T(8,128)} %shard_map.107), calls=%async_computation.1 | async-start | bytes 262144 | tf_op jit(solution)/shard_map/all_to_all | solution.py:29
  83.6 7.2 %collective-permute-start.9 = (bf16[4,896,128]{2,1,0:T(8,128)(2,1)S(1)}, bf16[4,896,128]{2,1,0:T(8,128)(2,1)}, u32[]{:S(2)}, u32[]{:S(2)}) collective-permute-start(bf16[4,896,128]{2,1,0:T(8,128)(2,1)S(1)} %bitcast.19), channel_id=1, source_target_pairs={{0,16},{16,0},{1,17},{17,1},{2,18},{18,2},{3,19},{19,3},{4,20},{20... | collective-permute-start | bytes 2752520 | tf_op jit(solution)/shard_map/ppermute | solution.py:25
  90.8 1.8 slice.8
  92.7 2.0 collective-permute-start.1
  94.7 1.8 slice.9
  96.5 13.9 %collective-permute-start.10 = (bf16[4,896,128]{2,1,0:T(8,128)(2,1)}, bf16[4,896,128]{2,1,0:T(8,128)(2,1)}, u32[]{:S(2)}, u32[]{:S(2)}) collective-permute-start(bf16[4,896,128]{2,1,0:T(8,128)(2,1)} %collective-permute-done.w1), channel_id=1, source_target_pairs={{0,16},{16,0},{1,17},{17,1},{2,18},{18,2},{3,19},{19,3},{4,20},{20... | collective-permute-start | bytes 2752520 | tf_op jit(solution)/shard_map/ppermute | solution.py:25
  110.4 1.9 collective-permute-start.11
  112.3 1.2 collective-permute-done.8.g3
  113.5 3.4 %collective-permute-start.3 = (bf16[2,896,128]{2,1,0:T(8,128)(2,1)}, bf16[2,896,128]{2,1,0:T(8,128)(2,1)S(1)}, u32[]{:S(2)}, u32[]{:S(2)}) collective-permute-start(bf16[2,896,128]{2,1,0:T(8,128)(2,1)} %slice.9), channel_id=1, source_target_pairs={{0,384},{128,0},{256,128},{384,256},{1,385},{129,1},{257,129},{385... | collective-permute-start | bytes 1376264 | tf_op jit(solution)/shard_map/ppermute | solution.py:25
  117.6 4.3 %all-to-all-start.2 = ((f32[16,16,128]{2,1,0:T(8,128)}), f32[16,16,128]{2,1,0:T(8,128)S(1)}, u32[]{:S(2)}, u32[]{:S(2)}) async-start(f32[16,16,128]{2,1,0:T(8,128)} %broadcast_in_dim.10), calls=%async_computation.2 | async-start | bytes 262144 | tf_op jit(solution)/shard_map/all_to_all | solution.py:29
  121.9 3.0 %collective-permute-start.4 = (bf16[2,896,128]{2,1,0:T(8,128)(2,1)}, bf16[2,896,128]{2,1,0:T(8,128)(2,1)S(1)}, u32[]{:S(2)}, u32[]{:S(2)}) collective-permute-start(bf16[2,896,128]{2,1,0:T(8,128)(2,1)} %collective-permute-done.1.q0), channel_id=1, source_target_pairs={{0,16},{16,0},{1,17},{17,1},{2,18},{18,2},{3,19},{19,3},{4,20},{20... | collective-permute-start | bytes 1376264 | tf_op jit(solution)/shard_map/ppermute | solution.py:25
  124.9 2.2 %collective-permute-done.3.q1 = bf16[2,896,128]{2,1,0:T(8,128)(2,1)S(1)} collective-permute-done((bf16[2,896,128]{2,1,0:T(8,128)(2,1)}, bf16[2,896,128]{2,1,0:T(8,128)(2,1)S(1)}, u32[]{:S(2)}, u32[]{:S(2)}) %collective-permute-start.3) | collective-permute-done | bytes 458784 | tf_op jit(solution)/shard_map/ppermute | solution.py:25
  127.1 3.3 %collective-permute-start.5 = (bf16[2,896,128]{2,1,0:T(8,128)(2,1)S(1)}, bf16[2,896,128]{2,1,0:T(8,128)(2,1)}, u32[]{:S(2)}, u32[]{:S(2)}) collective-permute-start(bf16[2,896,128]{2,1,0:T(8,128)(2,1)S(1)} %collective-permute-done.3.q1), channel_id=1, source_target_pairs={{0,16},{16,0},{1,17},{17,1},{2,18},{18,2},{3,19},{19,3},{4,20},{20... | collective-permute-start | bytes 1376264 | tf_op jit(solution)/shard_map/ppermute | solution.py:25
  130.5 2.8 %shard_map.105.slope_ref = f32[384,896]{1,0:T(8,128)} custom-call(bf16[384,896]{1,0:T(8,128)(2,1)} %gate_ref.1, bf16[384,896]{1,0:T(8,128)(2,1)} %up_ref.1), custom_call_target="tpu_custom_call" | custom-call | tf_op jit(solution)/shard_map/pallas_call | solution.py:211
  134.0 6.4 %shard_map.104.acc_ref = f32[384,896]{1,0:T(8,128)} custom-call(s32[6]{0:T(128)} %stack.27.where, bf16[4,896,128]{2,1,0:T(8,128)(2,1)} %bitcast.20, bf16[4,896,128]{2,1,0:T(8,128)(2,1)} %collective-permute-done.w1, bf16[4,896,128]{2,1,0:T(8,128)(2,1)} %collective-permute-done.2.w2, bf16[4,896,128]{2,1,0:T(8,128)(2,1)} %collective-permute-done.9.v0, ...), custom_call_target="tpu_custom_call" | custom-call | tf_op jit(solution)/shard_map/pallas_call | solution.py:219
  141.2 5.3 %shard_map.106 = f32[16,16,128]{2,1,0:T(8,128)} custom-call(s32[6]{0:T(128)} %stack.27.where, bf16[2,896,128]{2,1,0:T(8,128)(2,1)} %collective-permute-done.1.q0, bf16[2,896,128]{2,1,0:T(8,128)(2,1)} %copy-done.6, bf16[2,896,128]{2,1,0:T(8,128)(2,1)} %copy-done.7, bf16[2,896,128]{2,1,0:T(8,128)(2,1)} %collective-permute-done.5.r1, ...), custom_call_target="tpu_custom_call" | custom-call | tf_op jit(solution)/shard_map/pallas_call | solution.py:230
  146.6 12.5 %all_to_all.25.out_ref = f32[16,16,128]{2,1,0:T(8,128)} all-to-all(f32[16,16,128]{2,1,0:T(8,128)} %shard_map.106), channel_id=1, replica_groups=mesh['y'=4,'zh'=4,'c'=2,'zl'=4,'x'=4] {'zl','x'}, dimensions={0} | all-to-all | bytes 262144 | tf_op jit(solution)/shard_map/all_to_all | solution.py:29
  159.1 2.0 shard_map.108
  161.1 11.6 %all-to-all-start.3 = ((f32[32,8,128]{2,1,0:T(8,128)}), f32[32,8,128]{2,1,0:T(8,128)S(1)}, u32[]{:S(2)}, u32[]{:S(2)}) async-start(f32[32,8,128]{2,1,0:T(8,128)} %shard_map.108), calls=%async_computation.3 | async-start | bytes 262144 | tf_op jit(solution)/shard_map/all_to_all | solution.py:29
  173.4 15.1 %all-to-all-done.3.all_ref = f32[32,8,128]{2,1,0:T(8,128)S(1)} async-done(((f32[32,8,128]{2,1,0:T(8,128)}), f32[32,8,128]{2,1,0:T(8,128)S(1)}, u32[]{:S(2)}, u32[]{:S(2)}) %all-to-all-start.3) | async-done | bytes 131104 | tf_op jit(solution)/shard_map/all_to_all | solution.py:29
  189.1 2.1 shard_map.109
  191.2 18.5 %all_to_all.26.all_ref = bf16[16,112,128]{2,1,0:T(8,128)(2,1)} all-to-all(bf16[16,112,128]{2,1,0:T(8,128)(2,1)} %get-tuple-element.8), channel_id=1, replica_groups=mesh['y'=4,'zh'=4,'c'=2,'zl'=4,'x'=4] {'zl','x'}, dimensions={0} | all-to-all | bytes 917504 | tf_op jit(solution)/shard_map/all_to_all | solution.py:29
  209.7 2.0 shard_map.110
  211.7 1.3 copy.12
  (35 shorter events, 3.7 us)
Async XLA Ops:
  20.1 76.4 %copy-start = (bf16[1536,256]{1,0:T(8,128)(2,1)}, bf16[1536,256]{1,0:T(8,128)(2,1)S(1)}, u32[]{:S(2)}) copy-start(bf16[1536,256]{1,0:T(8,128)(2,1)S(1)} %all-gather) | copy-start | bytes 2359300
  61.6 56.0 %copy-start.1 = (bf16[3584,128]{1,0:T(8,128)(2,1)}, bf16[3584,128]{1,0:T(8,128)(2,1)S(1)}, u32[]{:S(2)}) copy-start(bf16[3584,128]{1,0:T(8,128)(2,1)S(1)} %all-gather.1) | copy-start | bytes 2752516
  61.6 22.0 %collective-permute-start = (bf16[4,896,128]{2,1,0:T(8,128)(2,1)S(1)}, bf16[4,896,128]{2,1,0:T(8,128)(2,1)}, u32[]{:S(2)}, u32[]{:S(2)}) collective-permute-start(bf16[4,896,128]{2,1,0:T(8,128)(2,1)S(1)} %bitcast.17), channel_id=1, source_target_pairs={{0,128},{128,256},{256,384},{384,0},{1,129},{129,257},{257,385},{3... | collective-permute-start | bytes 2752520 | tf_op jit(solution)/shard_map/ppermute | solution.py:25
  64.8 27.9 %collective-permute-start.2 = (bf16[4,896,128]{2,1,0:T(8,128)(2,1)S(1)}, bf16[4,896,128]{2,1,0:T(8,128)(2,1)}, u32[]{:S(2)}, u32[]{:S(2)}) collective-permute-start(bf16[4,896,128]{2,1,0:T(8,128)(2,1)S(1)} %bitcast.18), channel_id=1, source_target_pairs={{0,384},{128,0},{256,128},{384,256},{1,385},{129,1},{257,129},{385... | collective-permute-start | bytes 2752520 | tf_op jit(solution)/shard_map/ppermute | solution.py:25
  68.2 28.4 %collective-permute-start.6 = (bf16[4,384,256]{2,1,0:T(8,128)(2,1)S(1)}, bf16[4,384,256]{2,1,0:T(8,128)(2,1)S(1)}, u32[]{:S(2)}, u32[]{:S(2)}) collective-permute-start(bf16[4,384,256]{2,1,0:T(8,128)(2,1)S(1)} %bitcast.12), channel_id=1, source_target_pairs={{0,3},{1,0},{2,1},{3,2},{4,7},{5,4},{6,5},{7,6},{8,11},{9,8},{10,9... | collective-permute-start | bytes 2359304 | tf_op jit(solution)/shard_map/ppermute | solution.py:25
  72.5 37.8 %collective-permute-start.7 = (bf16[4,384,256]{2,1,0:T(8,128)(2,1)S(1)}, bf16[4,384,256]{2,1,0:T(8,128)(2,1)S(1)}, u32[]{:S(2)}, u32[]{:S(2)}) collective-permute-start(bf16[4,384,256]{2,1,0:T(8,128)(2,1)S(1)} %bitcast.13), channel_id=1, source_target_pairs={{0,2},{1,3},{2,0},{3,1},{4,6},{5,7},{6,4},{7,5},{8,10},{9,11},{10,... | collective-permute-start | bytes 2359304 | tf_op jit(solution)/shard_map/ppermute | solution.py:25
  75.0 38.5 %collective-permute-start.8 = (bf16[4,384,256]{2,1,0:T(8,128)(2,1)S(1)}, bf16[4,384,256]{2,1,0:T(8,128)(2,1)}, u32[]{:S(2)}, u32[]{:S(2)}) collective-permute-start(bf16[4,384,256]{2,1,0:T(8,128)(2,1)S(1)} %bitcast.14), channel_id=1, source_target_pairs={{0,1},{1,2},{2,3},{3,0},{4,5},{5,6},{6,7},{7,4},{8,9},{9,10},{10,1... | collective-permute-start | bytes 2359304 | tf_op jit(solution)/shard_map/ppermute | solution.py:25
  79.3 37.6 %all-to-all-start.1 = ((f32[16,16,128]{2,1,0:T(8,128)}), f32[16,16,128]{2,1,0:T(8,128)S(1)}, u32[]{:S(2)}, u32[]{:S(2)}) async-start(f32[16,16,128]{2,1,0:T(8,128)} %shard_map.107), calls=%async_computation.1 | async-start | bytes 262144 | tf_op jit(solution)/shard_map/all_to_all | solution.py:29
  83.6 50.4 %collective-permute-start.9 = (bf16[4,896,128]{2,1,0:T(8,128)(2,1)S(1)}, bf16[4,896,128]{2,1,0:T(8,128)(2,1)}, u32[]{:S(2)}, u32[]{:S(2)}) collective-permute-start(bf16[4,896,128]{2,1,0:T(8,128)(2,1)S(1)} %bitcast.19), channel_id=1, source_target_pairs={{0,16},{16,0},{1,17},{17,1},{2,18},{18,2},{3,19},{19,3},{4,20},{20... | collective-permute-start | bytes 2752520 | tf_op jit(solution)/shard_map/ppermute | solution.py:25
  92.7 29.2 %collective-permute-start.1 = (bf16[2,896,128]{2,1,0:T(8,128)(2,1)}, bf16[2,896,128]{2,1,0:T(8,128)(2,1)}, u32[]{:S(2)}, u32[]{:S(2)}) collective-permute-start(bf16[2,896,128]{2,1,0:T(8,128)(2,1)} %slice.8), channel_id=1, source_target_pairs={{0,128},{128,256},{256,384},{384,0},{1,129},{129,257},{257,385},{3... | collective-permute-start | bytes 1376264 | tf_op jit(solution)/shard_map/ppermute | solution.py:25
  96.5 36.8 %copy-start.2 = (bf16[4,384,256]{2,1,0:T(8,128)(2,1)}, bf16[4,384,256]{2,1,0:T(8,128)(2,1)S(1)}, u32[]{:S(2)}) copy-start(bf16[4,384,256]{2,1,0:T(8,128)(2,1)S(1)} %collective-permute-done.6.g1) | copy-start | bytes 2359300
  96.5 37.5 %collective-permute-start.10 = (bf16[4,896,128]{2,1,0:T(8,128)(2,1)}, bf16[4,896,128]{2,1,0:T(8,128)(2,1)}, u32[]{:S(2)}, u32[]{:S(2)}) collective-permute-start(bf16[4,896,128]{2,1,0:T(8,128)(2,1)} %collective-permute-done.w1), channel_id=1, source_target_pairs={{0,16},{16,0},{1,17},{17,1},{2,18},{18,2},{3,19},{19,3},{4,20},{20... | collective-permute-start | bytes 2752520 | tf_op jit(solution)/shard_map/ppermute | solution.py:25
  110.4 22.9 %copy-start.3 = (bf16[4,384,256]{2,1,0:T(8,128)(2,1)}, bf16[4,384,256]{2,1,0:T(8,128)(2,1)S(1)}, u32[]{:S(2)}) copy-start(bf16[4,384,256]{2,1,0:T(8,128)(2,1)S(1)} %collective-permute-done.7.g2) | copy-start | bytes 2359300
  110.4 23.6 %collective-permute-start.11 = (bf16[4,896,128]{2,1,0:T(8,128)(2,1)}, bf16[4,896,128]{2,1,0:T(8,128)(2,1)}, u32[]{:S(2)}, u32[]{:S(2)}) collective-permute-start(bf16[4,896,128]{2,1,0:T(8,128)(2,1)} %collective-permute-done.2.w2), channel_id=1, source_target_pairs={{0,16},{16,0},{1,17},{17,1},{2,18},{18,2},{3,19},{19,3},{4,20},{20... | collective-permute-start | bytes 2752520 | tf_op jit(solution)/shard_map/ppermute | solution.py:25
  113.5 13.6 %collective-permute-start.3 = (bf16[2,896,128]{2,1,0:T(8,128)(2,1)}, bf16[2,896,128]{2,1,0:T(8,128)(2,1)S(1)}, u32[]{:S(2)}, u32[]{:S(2)}) collective-permute-start(bf16[2,896,128]{2,1,0:T(8,128)(2,1)} %slice.9), channel_id=1, source_target_pairs={{0,384},{128,0},{256,128},{384,256},{1,385},{129,1},{257,129},{385... | collective-permute-start | bytes 1376264 | tf_op jit(solution)/shard_map/ppermute | solution.py:25
  117.6 29.0 %all-to-all-start.2 = ((f32[16,16,128]{2,1,0:T(8,128)}), f32[16,16,128]{2,1,0:T(8,128)S(1)}, u32[]{:S(2)}, u32[]{:S(2)}) async-start(f32[16,16,128]{2,1,0:T(8,128)} %broadcast_in_dim.10), calls=%async_computation.2 | async-start | bytes 262144 | tf_op jit(solution)/shard_map/all_to_all | solution.py:29
  121.9 18.5 %collective-permute-start.4 = (bf16[2,896,128]{2,1,0:T(8,128)(2,1)}, bf16[2,896,128]{2,1,0:T(8,128)(2,1)S(1)}, u32[]{:S(2)}, u32[]{:S(2)}) collective-permute-start(bf16[2,896,128]{2,1,0:T(8,128)(2,1)} %collective-permute-done.1.q0), channel_id=1, source_target_pairs={{0,16},{16,0},{1,17},{17,1},{2,18},{18,2},{3,19},{19,3},{4,20},{20... | collective-permute-start | bytes 1376264 | tf_op jit(solution)/shard_map/ppermute | solution.py:25
  127.1 6.2 %copy-start.6 = (bf16[2,896,128]{2,1,0:T(8,128)(2,1)}, bf16[2,896,128]{2,1,0:T(8,128)(2,1)S(1)}, u32[]{:S(2)}) copy-start(bf16[2,896,128]{2,1,0:T(8,128)(2,1)S(1)} %collective-permute-done.3.q1) | copy-start | bytes 1376260
  127.1 13.3 %collective-permute-start.5 = (bf16[2,896,128]{2,1,0:T(8,128)(2,1)S(1)}, bf16[2,896,128]{2,1,0:T(8,128)(2,1)}, u32[]{:S(2)}, u32[]{:S(2)}) collective-permute-start(bf16[2,896,128]{2,1,0:T(8,128)(2,1)S(1)} %collective-permute-done.3.q1), channel_id=1, source_target_pairs={{0,16},{16,0},{1,17},{17,1},{2,18},{18,2},{3,19},{19,3},{4,20},{20... | collective-permute-start | bytes 1376264 | tf_op jit(solution)/shard_map/ppermute | solution.py:25
  140.4 0.8 copy-start.7
  141.2 31.5 %copy-start.8 = (s32[16]{0:T(128)S(1)}, s32[16]{0:T(128)}, u32[]{:S(2)}) copy-start(s32[16]{0:T(128)} %param.17) | copy-start | bytes 196
  146.6 12.5 %copy-start.4 = (f32[16,16,128]{2,1,0:T(8,128)}, f32[16,16,128]{2,1,0:T(8,128)S(1)}, u32[]{:S(2)}) copy-start(f32[16,16,128]{2,1,0:T(8,128)S(1)} %all-to-all-done.2.in_ref) | copy-start | bytes 393220
  161.1 27.4 %all-to-all-start.3 = ((f32[32,8,128]{2,1,0:T(8,128)}), f32[32,8,128]{2,1,0:T(8,128)S(1)}, u32[]{:S(2)}, u32[]{:S(2)}) async-start(f32[32,8,128]{2,1,0:T(8,128)} %shard_map.108), calls=%async_computation.3 | async-start | bytes 262144 | tf_op jit(solution)/shard_map/all_to_all | solution.py:29
  188.5 0.7 copy-start.5

commit v2 on v1

--- a/solution.py
+++ b/solution.py
@@ -15,6 +15,8 @@
 BF16 = jnp.bfloat16
 HIGH = lax.Precision.HIGHEST
 NT = (((1,), (1,)), ((), ()))
+SMALL = pltpu.CompilerParams(vmem_limit_bytes=8 << 20)
+LARGE = pltpu.CompilerParams(vmem_limit_bytes=24 << 20)
 VM = pl.BlockSpec(memory_space=pltpu.VMEM)
 SM = pl.BlockSpec(memory_space=pltpu.SMEM)
 ANY = pl.BlockSpec(memory_space=pl.ANY)
@@ -176,7 +178,7 @@
         rows, cols, (((0,), (0,)), ((), ())), precision=HIGH, preferred_element_type=F32
     )
     gram_ref[...] = block * (width * all_ref.shape[0] / count) / norm
-    score_ref[...] = (score / norm)[:, :examples]
+    score_ref[...] = (score / norm).T[:examples]
 
 
 def step(acts, grad_out, gate_pre, up_pre, down_weight, proj_in, proj_out, lengths, query_ids):
@@ -200,17 +202,20 @@
     wm = shift(wz, "y", -1)
     q0 = shift(wp[:2], "y", 1)
     q1 = shift(wm[2:], "y", -1)
-    cz, cp, cm = shift(wz, "c", 1), shift(wp, "c", 1), shift(wm, "c", 1)
+    cz = shift(wz, "c", 1)
+    cp = shift(wp, "c", 1)
+    cm = shift(wm, "c", 1)
     r0, r1 = shift(q0, "c", 1), shift(q1, "c", 1)
 
     in_msg = pl.pallas_call(
-        functools.partial(in_kernel, examples, per), out_shape=msg, in_specs=[VM, VM], out_specs=VM
+        functools.partial(in_kernel, examples, per), out_shape=msg, in_specs=[VM, VM], out_specs=VM, compiler_params=SMALL
     )(proj_in.T, acts)
     in_own = jnp.sum(exchange(in_msg, TENSOR), axis=0)
     in_all = exchange(jnp.broadcast_to(in_own[None], (tensor, *in_own.shape)), TENSOR)
     slope = pl.pallas_call(
         slope_kernel,
         out_shape=jax.ShapeDtypeStruct((tokens, ff_here), F32),
+        compiler_params=SMALL,
         in_specs=[VM, VM],
         out_specs=VM,
     )(gate_pre, up_pre)
@@ -219,6 +224,7 @@
     acc = pl.pallas_call(
         most_kernel,
         out_shape=jax.ShapeDtypeStruct((tokens, ff_here), F32),
+        compiler_params=LARGE,
         in_specs=[SM] + [ANY] * 10,
         out_specs=VM,
         scratch_shapes=[
@@ -230,6 +236,7 @@
     out_msg = pl.pallas_call(
         functools.partial(last_kernel, examples, per),
         out_shape=msg,
+        compiler_params=LARGE,
         in_specs=[SM] + [ANY] * 8 + [VM] * 3,
         out_specs=VM,
         scratch_shapes=[
@@ -242,6 +249,7 @@
     piece = pl.pallas_call(
         functools.partial(feature_kernel, examples, per),
         out_shape=jax.ShapeDtypeStruct((groups, 8, 128), F32),
+        compiler_params=SMALL,
         in_specs=[SM, VM, VM],
         out_specs=VM,
     )(lengths, out_all, in_all)
@@ -255,6 +263,7 @@
             jax.ShapeDtypeStruct((count, 256), F32),
             jax.ShapeDtypeStruct((tensor, count + queries, 128), BF16),
         ),
+        compiler_params=SMALL,
         in_specs=[SM, VM, VM],
         out_specs=(VM, VM),
     )(where, pick, pieces)
@@ -263,12 +272,13 @@
         functools.partial(gram_kernel, examples),
         out_shape=(
             jax.ShapeDtypeStruct((128, 256), F32),
-            jax.ShapeDtypeStruct((queries, examples), F32),
+            jax.ShapeDtypeStruct((examples, queries), F32),
         ),
+        compiler_params=SMALL,
         in_specs=[SM, VM, VM],
         out_specs=(VM, VM),
     )(where, row_all, cols)
-    return gram, scores
+    return gram, scores.T
 
 
 def solution(mesh):

time: 214 us -> 207 us (0.967)
  Pallas kernels: 22.5 us -> 14.1 us
    unnamed x18, local copies, waits for them, and re-layouts: 1.42 us -> 4.25 us
    pallas_call x1, Pallas kernels: 2.84 us -> 0.42 us  [step(): pl.pallas_call(slope_kernel, out_shape=jax.ShapeDtypeStruct((tokens, ff_h...]
  transfers between devices with their start and end apart: 15 -> 15, of which waited for: 4 -> 4; matrix products, arithmetic and copies ran while one was open for 3% -> 2% of each run, Pallas kernels for 8% -> 5%
where the time goes in v2:
time: 207 us; the launch traced here: 206 us
  blocking collectives  92.4 us (45%)
  starting transfers between devices  72.2 us (35%)
  waiting for transfers between devices  18.5 us (9%)
  Pallas kernels  14.1 us (7%)
  local copies, waits for them, and re-layouts  8 us (4%)
    ppermute x12, starting transfers between devices, shift(): lax.ppermute(value, axis, [(k, (k + by) % count) for k in range(count)])  51.3 us
    all_gather x1, blocking collectives, step(): wz = lax.all_gather(down_weight, 'zh')  41.5 us
    all_to_all x2, blocking collectives, exchange(): return lax.all_to_all(value, axis, 0, 0, tiled=True)  31.3 us
    all_to_all x3, starting transfers between devices, exchange(): return lax.all_to_all(value, axis, 0, 0, tiled=True)  21 us
    all_gather x1, blocking collectives, step(): gz = lax.all_gather(grad_out, 'zl')  19.6 us
    all_to_all x3, waiting for transfers between devices, exchange(): return lax.all_to_all(value, axis, 0, 0, tiled=True)  15.7 us
    pallas_call x1, Pallas kernels, step(): pl.pallas_call(most_kernel, out_shape=jax.ShapeDtypeStruct((tokens, ff_he...  5.31 us
    unnamed x18, local copies, waits for them, and re-layouts  4.25 us
  transfers between devices with their start and end apart: 15, of which 4 were waited for; matrix products, arithmetic and copies ran while one was open for 2% of the time, Pallas kernels for 5%

profile of v2, /device:TPU:1, one launch (start us, length us, event | category | flops | bytes accessed | tf_op | source)
XLA Modules:
  0.0 206.2 jit_solution(3618989730776716153)
XLA Ops:
  0.6 19.6 %all-gather = bf16[1536,256]{1,0:T(8,128)(2,1)S(1)} all-gather(bf16[384,256]{1,0:T(8,128)(2,1)} %param.10), channel_id=2, replica_groups=mesh['y'=4,'zh'=4,'c'=2,'zl'=4,'x'=4] {'zl'}, dimensions={0}, use_global_device_ids=true | all-gather | bytes 983040 | tf_op jit(solution)/shard_map/all_gather | solution.py:195
  20.2 41.5 %all-gather.1 = bf16[3584,128]{1,0:T(8,128)(2,1)S(1)} all-gather(bf16[896,128]{1,0:T(8,128)(2,1)} %param.13), channel_id=3, replica_groups=mesh['y'=4,'zh'=4,'c'=2,'zl'=4,'x'=4] {'zh'}, dimensions={0}, use_global_device_ids=true | all-gather | bytes 1146880 | tf_op jit(solution)/shard_map/all_gather | solution.py:197
  61.7 3.2 %collective-permute-start = (bf16[4,896,128]{2,1,0:T(8,128)(2,1)S(1)}, bf16[4,896,128]{2,1,0:T(8,128)(2,1)}, u32[]{:S(2)}, u32[]{:S(2)}) collective-permute-start(bf16[4,896,128]{2,1,0:T(8,128)(2,1)S(1)} %bitcast.18), channel_id=1, source_target_pairs={{0,128},{128,256},{256,384},{384,0},{1,129},{129,257},{257,385},{3... | collective-permute-start | bytes 2752520 | tf_op jit(solution)/shard_map/ppermute | solution.py:27
  64.9 3.4 %collective-permute-start.2 = (bf16[4,896,128]{2,1,0:T(8,128)(2,1)S(1)}, bf16[4,896,128]{2,1,0:T(8,128)(2,1)}, u32[]{:S(2)}, u32[]{:S(2)}) collective-permute-start(bf16[4,896,128]{2,1,0:T(8,128)(2,1)S(1)} %bitcast.19), channel_id=1, source_target_pairs={{0,384},{128,0},{256,128},{384,256},{1,385},{129,1},{257,129},{385... | collective-permute-start | bytes 2752520 | tf_op jit(solution)/shard_map/ppermute | solution.py:27
  68.3 4.4 %collective-permute-start.6 = (bf16[4,384,256]{2,1,0:T(8,128)(2,1)S(1)}, bf16[4,384,256]{2,1,0:T(8,128)(2,1)S(1)}, u32[]{:S(2)}, u32[]{:S(2)}) collective-permute-start(bf16[4,384,256]{2,1,0:T(8,128)(2,1)S(1)} %bitcast.13), channel_id=1, source_target_pairs={{0,3},{1,0},{2,1},{3,2},{4,7},{5,4},{6,5},{7,6},{8,11},{9,8},{10,9... | collective-permute-start | bytes 2359304 | tf_op jit(solution)/shard_map/ppermute | solution.py:27
  72.7 2.4 %collective-permute-start.7 = (bf16[4,384,256]{2,1,0:T(8,128)(2,1)S(1)}, bf16[4,384,256]{2,1,0:T(8,128)(2,1)}, u32[]{:S(2)}, u32[]{:S(2)}) collective-permute-start(bf16[4,384,256]{2,1,0:T(8,128)(2,1)S(1)} %bitcast.14), channel_id=1, source_target_pairs={{0,2},{1,3},{2,0},{3,1},{4,6},{5,7},{6,4},{7,5},{8,10},{9,11},{10,... | collective-permute-start | bytes 2359304 | tf_op jit(solution)/shard_map/ppermute | solution.py:27
  75.1 2.5 %collective-permute-start.8 = (bf16[4,384,256]{2,1,0:T(8,128)(2,1)S(1)}, bf16[4,384,256]{2,1,0:T(8,128)(2,1)}, u32[]{:S(2)}, u32[]{:S(2)}) collective-permute-start(bf16[4,384,256]{2,1,0:T(8,128)(2,1)S(1)} %bitcast.15), channel_id=1, source_target_pairs={{0,1},{1,2},{2,3},{3,0},{4,5},{5,6},{6,7},{7,4},{8,9},{9,10},{10,1... | collective-permute-start | bytes 2359304 | tf_op jit(solution)/shard_map/ppermute | solution.py:27
  78.5 4.2 %all-to-all-start.1 = ((f32[16,16,128]{2,1,0:T(8,128)}), f32[16,16,128]{2,1,0:T(8,128)S(1)}, u32[]{:S(2)}, u32[]{:S(2)}) async-start(f32[16,16,128]{2,1,0:T(8,128)} %shard_map.107), calls=%async_computation.1 | async-start | bytes 262144 | tf_op jit(solution)/shard_map/all_to_all | solution.py:31
  82.7 1.1 collective-permute-done.w1
  83.8 6.3 %collective-permute-start.9 = (bf16[4,896,128]{2,1,0:T(8,128)(2,1)S(1)}, bf16[4,896,128]{2,1,0:T(8,128)(2,1)}, u32[]{:S(2)}, u32[]{:S(2)}) collective-permute-start(bf16[4,896,128]{2,1,0:T(8,128)(2,1)S(1)} %bitcast.20), channel_id=1, source_target_pairs={{0,16},{16,0},{1,17},{17,1},{2,18},{18,2},{3,19},{19,3},{4,20},{20... | collective-permute-start | bytes 2752520 | tf_op jit(solution)/shard_map/ppermute | solution.py:27
  90.1 1.1 slice.8
  91.1 2.0 collective-permute-start.1
  93.1 1.9 slice.9
  95.9 15.5 %collective-permute-start.10 = (bf16[4,896,128]{2,1,0:T(8,128)(2,1)}, bf16[4,896,128]{2,1,0:T(8,128)(2,1)}, u32[]{:S(2)}, u32[]{:S(2)}) collective-permute-start(bf16[4,896,128]{2,1,0:T(8,128)(2,1)} %collective-permute-done.w1), channel_id=1, source_target_pairs={{0,16},{16,0},{1,17},{17,1},{2,18},{18,2},{3,19},{19,3},{4,20},{20... | collective-permute-start | bytes 2752520 | tf_op jit(solution)/shard_map/ppermute | solution.py:27
  111.5 1.9 collective-permute-start.11
  113.7 3.4 %collective-permute-start.3 = (bf16[2,896,128]{2,1,0:T(8,128)(2,1)}, bf16[2,896,128]{2,1,0:T(8,128)(2,1)}, u32[]{:S(2)}, u32[]{:S(2)}) collective-permute-start(bf16[2,896,128]{2,1,0:T(8,128)(2,1)} %slice.9), channel_id=1, source_target_pairs={{0,384},{128,0},{256,128},{384,256},{1,385},{129,1},{257,129},{385... | collective-permute-start | bytes 1376264 | tf_op jit(solution)/shard_map/ppermute | solution.py:27
  117.7 5.2 %all-to-all-start.2 = ((f32[16,16,128]{2,1,0:T(8,128)}), f32[16,16,128]{2,1,0:T(8,128)S(1)}, u32[]{:S(2)}, u32[]{:S(2)}) async-start(f32[16,16,128]{2,1,0:T(8,128)} %broadcast_in_dim.10), calls=%async_computation.2 | async-start | bytes 262144 | tf_op jit(solution)/shard_map/all_to_all | solution.py:31
  123.0 3.0 %collective-permute-start.4 = (bf16[2,896,128]{2,1,0:T(8,128)(2,1)}, bf16[2,896,128]{2,1,0:T(8,128)(2,1)}, u32[]{:S(2)}, u32[]{:S(2)}) collective-permute-start(bf16[2,896,128]{2,1,0:T(8,128)(2,1)} %collective-permute-done.1.q0), channel_id=1, source_target_pairs={{0,16},{16,0},{1,17},{17,1},{2,18},{18,2},{3,19},{19,3},{4,20},{20... | collective-permute-start | bytes 1376264 | tf_op jit(solution)/shard_map/ppermute | solution.py:27
  125.9 1.4 collective-permute-done.3.q1
  127.4 3.3 %collective-permute-start.5 = (bf16[2,896,128]{2,1,0:T(8,128)(2,1)}, bf16[2,896,128]{2,1,0:T(8,128)(2,1)}, u32[]{:S(2)}, u32[]{:S(2)}) collective-permute-start(bf16[2,896,128]{2,1,0:T(8,128)(2,1)} %collective-permute-done.3.q1), channel_id=1, source_target_pairs={{0,16},{16,0},{1,17},{17,1},{2,18},{18,2},{3,19},{19,3},{4,20},{20... | collective-permute-start | bytes 1376264 | tf_op jit(solution)/shard_map/ppermute | solution.py:27
  130.7 1.1 copy-done.2
  131.8 1.1 copy-done.3
  133.5 1.1 copy-done.1
  134.6 5.3 %shard_map.104.acc_ref = f32[384,896]{1,0:T(8,128)S(1)} custom-call(s32[6]{0:T(128)S(1)} %stack.27.where, bf16[4,896,128]{2,1,0:T(8,128)(2,1)S(1)} %bitcast.21, bf16[4,896,128]{2,1,0:T(8,128)(2,1)} %collective-permute-done.w1, bf16[4,896,128]{2,1,0:T(8,128)(2,1)} %collective-permute-done.2.w2, bf16[4,896,128]{2,1,0:T(8,128)(2,1)} %collective-permute-done.9.v0, ...), custom_call_target="tpu_custom_call" | custom-call | tf_op jit(solution)/shard_map/pallas_call | solution.py:224
  140.0 3.5 %shard_map.106 = f32[16,16,128]{2,1,0:T(8,128)S(1)} custom-call(s32[6]{0:T(128)S(1)} %stack.27.where, bf16[2,896,128]{2,1,0:T(8,128)(2,1)} %collective-permute-done.1.q0, bf16[2,896,128]{2,1,0:T(8,128)(2,1)} %collective-permute-done.3.q1, bf16[2,896,128]{2,1,0:T(8,128)(2,1)} %collective-permute-done.4.r0, bf16[2,896,128]{2,1,0:T(8,128)(2,1)} %collective-permute-done.5.r1, ...), custom_call_target="tpu_custom_call" | custom-call | tf_op jit(solution)/shard_map/pallas_call | solution.py:236
  143.5 13.1 %all_to_all.25.out_ref = f32[16,16,128]{2,1,0:T(8,128)S(1)} all-to-all(f32[16,16,128]{2,1,0:T(8,128)S(1)} %shard_map.106), channel_id=1, replica_groups=mesh['y'=4,'zh'=4,'c'=2,'zl'=4,'x'=4] {'zl','x'}, dimensions={0} | all-to-all | bytes 262144 | tf_op jit(solution)/shard_map/all_to_all | solution.py:31
  156.6 1.5 shard_map.108
  158.2 11.5 %all-to-all-start.3 = ((f32[32,8,128]{2,1,0:T(8,128)}), f32[32,8,128]{2,1,0:T(8,128)S(1)}, u32[]{:S(2)}, u32[]{:S(2)}) async-start(f32[32,8,128]{2,1,0:T(8,128)} %shard_map.108), calls=%async_computation.3 | async-start | bytes 262144 | tf_op jit(solution)/shard_map/all_to_all | solution.py:31
  169.8 15.7 %all-to-all-done.3.all_ref = f32[32,8,128]{2,1,0:T(8,128)S(1)} async-done(((f32[32,8,128]{2,1,0:T(8,128)}), f32[32,8,128]{2,1,0:T(8,128)S(1)}, u32[]{:S(2)}, u32[]{:S(2)}) %all-to-all-start.3) | async-done | bytes 131104 | tf_op jit(solution)/shard_map/all_to_all | solution.py:31
  185.6 0.9 shard_map.109
  186.5 18.2 %all_to_all.26.all_ref = bf16[16,112,128]{2,1,0:T(8,128)(2,1)S(1)} all-to-all(bf16[16,112,128]{2,1,0:T(8,128)(2,1)S(1)} %get-tuple-element.10), channel_id=1, replica_groups=mesh['y'=4,'zh'=4,'c'=2,'zl'=4,'x'=4] {'zl','x'}, dimensions={0} | all-to-all | bytes 917504 | tf_op jit(solution)/shard_map/all_to_all | solution.py:31
  204.6 1.5 shard_map.110
  (34 shorter events, 3.4 us)
Async XLA Ops:
  0.6 77.0 %copy-start.6 = (bf16[256,64]{0,1:T(8,128)(2,1)S(1)}, bf16[256,64]{0,1:T(8,128)(2,1)}, u32[]{:S(2)}) copy-start(bf16[256,64]{0,1:T(8,128)(2,1)} %param.14) | copy-start | bytes 98308
  0.6 77.0 %copy-start.4 = (bf16[384,256]{1,0:T(8,128)(2,1)S(1)}, bf16[384,256]{1,0:T(8,128)(2,1)}, u32[]{:S(2)}) copy-start(bf16[384,256]{1,0:T(8,128)(2,1)} %acts_ref.1) | copy-start | bytes 589828
  61.7 22.0 %collective-permute-start = (bf16[4,896,128]{2,1,0:T(8,128)(2,1)S(1)}, bf16[4,896,128]{2,1,0:T(8,128)(2,1)}, u32[]{:S(2)}, u32[]{:S(2)}) collective-permute-start(bf16[4,896,128]{2,1,0:T(8,128)(2,1)S(1)} %bitcast.18), channel_id=1, source_target_pairs={{0,128},{128,256},{256,384},{384,0},{1,129},{129,257},{257,385},{3... | collective-permute-start | bytes 2752520 | tf_op jit(solution)/shard_map/ppermute | solution.py:27
  64.9 26.2 %collective-permute-start.2 = (bf16[4,896,128]{2,1,0:T(8,128)(2,1)S(1)}, bf16[4,896,128]{2,1,0:T(8,128)(2,1)}, u32[]{:S(2)}, u32[]{:S(2)}) collective-permute-start(bf16[4,896,128]{2,1,0:T(8,128)(2,1)S(1)} %bitcast.19), channel_id=1, source_target_pairs={{0,384},{128,0},{256,128},{384,256},{1,385},{129,1},{257,129},{385... | collective-permute-start | bytes 2752520 | tf_op jit(solution)/shard_map/ppermute | solution.py:27
  68.3 26.7 %collective-permute-start.6 = (bf16[4,384,256]{2,1,0:T(8,128)(2,1)S(1)}, bf16[4,384,256]{2,1,0:T(8,128)(2,1)S(1)}, u32[]{:S(2)}, u32[]{:S(2)}) collective-permute-start(bf16[4,384,256]{2,1,0:T(8,128)(2,1)S(1)} %bitcast.13), channel_id=1, source_target_pairs={{0,3},{1,0},{2,1},{3,2},{4,7},{5,4},{6,5},{7,6},{8,11},{9,8},{10,9... | collective-permute-start | bytes 2359304 | tf_op jit(solution)/shard_map/ppermute | solution.py:27
  72.7 38.8 %collective-permute-start.7 = (bf16[4,384,256]{2,1,0:T(8,128)(2,1)S(1)}, bf16[4,384,256]{2,1,0:T(8,128)(2,1)}, u32[]{:S(2)}, u32[]{:S(2)}) collective-permute-start(bf16[4,384,256]{2,1,0:T(8,128)(2,1)S(1)} %bitcast.14), channel_id=1, source_target_pairs={{0,2},{1,3},{2,0},{3,1},{4,6},{5,7},{6,4},{7,5},{8,10},{9,11},{10,... | collective-permute-start | bytes 2359304 | tf_op jit(solution)/shard_map/ppermute | solution.py:27
  75.1 38.5 %collective-permute-start.8 = (bf16[4,384,256]{2,1,0:T(8,128)(2,1)S(1)}, bf16[4,384,256]{2,1,0:T(8,128)(2,1)}, u32[]{:S(2)}, u32[]{:S(2)}) collective-permute-start(bf16[4,384,256]{2,1,0:T(8,128)(2,1)S(1)} %bitcast.15), channel_id=1, source_target_pairs={{0,1},{1,2},{2,3},{3,0},{4,5},{5,6},{6,7},{7,4},{8,9},{9,10},{10,1... | collective-permute-start | bytes 2359304 | tf_op jit(solution)/shard_map/ppermute | solution.py:27
  78.5 38.5 %all-to-all-start.1 = ((f32[16,16,128]{2,1,0:T(8,128)}), f32[16,16,128]{2,1,0:T(8,128)S(1)}, u32[]{:S(2)}, u32[]{:S(2)}) async-start(f32[16,16,128]{2,1,0:T(8,128)} %shard_map.107), calls=%async_computation.1 | async-start | bytes 262144 | tf_op jit(solution)/shard_map/all_to_all | solution.py:31
  83.8 49.7 %collective-permute-start.9 = (bf16[4,896,128]{2,1,0:T(8,128)(2,1)S(1)}, bf16[4,896,128]{2,1,0:T(8,128)(2,1)}, u32[]{:S(2)}, u32[]{:S(2)}) collective-permute-start(bf16[4,896,128]{2,1,0:T(8,128)(2,1)S(1)} %bitcast.20), channel_id=1, source_target_pairs={{0,16},{16,0},{1,17},{17,1},{2,18},{18,2},{3,19},{19,3},{4,20},{20... | collective-permute-start | bytes 2752520 | tf_op jit(solution)/shard_map/ppermute | solution.py:27
  91.1 31.8 %collective-permute-start.1 = (bf16[2,896,128]{2,1,0:T(8,128)(2,1)S(1)}, bf16[2,896,128]{2,1,0:T(8,128)(2,1)}, u32[]{:S(2)}, u32[]{:S(2)}) collective-permute-start(bf16[2,896,128]{2,1,0:T(8,128)(2,1)S(1)} %slice.8), channel_id=1, source_target_pairs={{0,128},{128,256},{256,384},{384,0},{1,129},{129,257},{257,385},{3... | collective-permute-start | bytes 1376264 | tf_op jit(solution)/shard_map/ppermute | solution.py:27
  95.0 0.9 copy-start
  95.9 37.5 %collective-permute-start.10 = (bf16[4,896,128]{2,1,0:T(8,128)(2,1)}, bf16[4,896,128]{2,1,0:T(8,128)(2,1)}, u32[]{:S(2)}, u32[]{:S(2)}) collective-permute-start(bf16[4,896,128]{2,1,0:T(8,128)(2,1)} %collective-permute-done.w1), channel_id=1, source_target_pairs={{0,16},{16,0},{1,17},{17,1},{2,18},{18,2},{3,19},{19,3},{4,20},{20... | collective-permute-start | bytes 2752520 | tf_op jit(solution)/shard_map/ppermute | solution.py:27
  111.5 22.0 %collective-permute-start.11 = (bf16[4,896,128]{2,1,0:T(8,128)(2,1)}, bf16[4,896,128]{2,1,0:T(8,128)(2,1)}, u32[]{:S(2)}, u32[]{:S(2)}) collective-permute-start(bf16[4,896,128]{2,1,0:T(8,128)(2,1)} %collective-permute-done.2.w2), channel_id=1, source_target_pairs={{0,16},{16,0},{1,17},{17,1},{2,18},{18,2},{3,19},{19,3},{4,20},{20... | collective-permute-start | bytes 2752520 | tf_op jit(solution)/shard_map/ppermute | solution.py:27
  113.7 13.7 %collective-permute-start.3 = (bf16[2,896,128]{2,1,0:T(8,128)(2,1)}, bf16[2,896,128]{2,1,0:T(8,128)(2,1)}, u32[]{:S(2)}, u32[]{:S(2)}) collective-permute-start(bf16[2,896,128]{2,1,0:T(8,128)(2,1)} %slice.9), channel_id=1, source_target_pairs={{0,384},{128,0},{256,128},{384,256},{1,385},{129,1},{257,129},{385... | collective-permute-start | bytes 1376264 | tf_op jit(solution)/shard_map/ppermute | solution.py:27
  117.7 25.8 %all-to-all-start.2 = ((f32[16,16,128]{2,1,0:T(8,128)}), f32[16,16,128]{2,1,0:T(8,128)S(1)}, u32[]{:S(2)}, u32[]{:S(2)}) async-start(f32[16,16,128]{2,1,0:T(8,128)} %broadcast_in_dim.10), calls=%async_computation.2 | async-start | bytes 262144 | tf_op jit(solution)/shard_map/all_to_all | solution.py:31
  123.0 16.9 %collective-permute-start.4 = (bf16[2,896,128]{2,1,0:T(8,128)(2,1)}, bf16[2,896,128]{2,1,0:T(8,128)(2,1)}, u32[]{:S(2)}, u32[]{:S(2)}) collective-permute-start(bf16[2,896,128]{2,1,0:T(8,128)(2,1)} %collective-permute-done.1.q0), channel_id=1, source_target_pairs={{0,16},{16,0},{1,17},{17,1},{2,18},{18,2},{3,19},{19,3},{4,20},{20... | collective-permute-start | bytes 1376264 | tf_op jit(solution)/shard_map/ppermute | solution.py:27
  127.4 12.6 %collective-permute-start.5 = (bf16[2,896,128]{2,1,0:T(8,128)(2,1)}, bf16[2,896,128]{2,1,0:T(8,128)(2,1)}, u32[]{:S(2)}, u32[]{:S(2)}) collective-permute-start(bf16[2,896,128]{2,1,0:T(8,128)(2,1)} %collective-permute-done.3.q1), channel_id=1, source_target_pairs={{0,16},{16,0},{1,17},{17,1},{2,18},{18,2},{3,19},{19,3},{4,20},{20... | collective-permute-start | bytes 1376264 | tf_op jit(solution)/shard_map/ppermute | solution.py:27
  130.7 1.1 copy-start.2
  131.8 1.1 copy-start.3
  133.4 1.1 copy-start.1
  134.6 5.3 %copy-start.5 = (bf16[896,64]{0,1:T(8,128)(2,1)S(1)}, bf16[896,64]{0,1:T(8,128)(2,1)}, u32[]{:S(2)}) copy-start(bf16[896,64]{0,1:T(8,128)(2,1)} %param.15) | copy-start | bytes 344068
  139.9 16.7 %copy-start.7 = (s32[3]{0:T(128)S(1)}, s32[3]{0:T(128)}, u32[]{:S(2)}) copy-start(s32[3]{0:T(128)} %lengths.1) | copy-start | bytes 40
  139.9 29.8 %copy-start.8 = (s32[16]{0:T(128)S(1)}, s32[16]{0:T(128)}, u32[]{:S(2)}) copy-start(s32[16]{0:T(128)} %param.17) | copy-start | bytes 196
  158.2 27.4 %all-to-all-start.3 = ((f32[32,8,128]{2,1,0:T(8,128)}), f32[32,8,128]{2,1,0:T(8,128)S(1)}, u32[]{:S(2)}, u32[]{:S(2)}) async-start(f32[32,8,128]{2,1,0:T(8,128)} %shard_map.108), calls=%async_computation.3 | async-start | bytes 262144 | tf_op jit(solution)/shard_map/all_to_all | solution.py:31
